TPU v7x, 32 devices: a whole 2x2x4 slice. The times are simulated.
32 devices in a mesh: groups: 2 (over y), section: 4 (over z), tensor: 4 (over x, core).
Axes of the slice: x: 2, y: 2, z: 4, core: 2. Of those that a mesh axis runs over, the one named last changes fastest.
Arguments:
- images: bfloat16 [2, 32, 3072], P('groups', None, 'tensor'), parts along dimension 0, may hold values from -6 to 6
- w_qkv: bfloat16 [4, 3, 3072, 3072], P('section', None, None, 'tensor'), may hold values from -0.109375 to 0.109375
- qk_gain: float32 [4, 2, 3072], P('section', None, 'tensor'), may hold values from 0.1 to 1.9
- w_out: bfloat16 [4, 3072, 3072], P('section', None, 'tensor'), may hold values from -0.109375 to 0.109375
- in_gain: float32 [4, 3072], P('section'), may hold values from 0.1 to 1.9
- out_gain: float32 [3072], P('tensor'), may hold values from 0.1 to 1.9
Outputs:
- pooled: float32 [4, 2, 3072], P('section', 'groups', 'tensor'), parts along dimension 1
There are 2 independent parts, one for each index of `groups`. A program takes and returns all parts, laid end to end along the dimension named above; an argument that names none is the same for every part. Nothing has to cross between parts.
All inputs are finite; a program needn't handle non-finite values.
Results may differ from a plain program's by a relative error of at most 0.015.
Values may be sent and summed in bfloat16 or wider, within the bound.
A program may use at most 64 MiB of HBM per device.

v0:
```python
import jax
import jax.numpy as jnp
from jax import lax
from jax.sharding import PartitionSpec as P

HEAD = 64


def shifted(block, axis, distance):
    devices = range(lax.axis_size(axis))
    route = [(i - distance, i) for i in devices if i - distance in devices]
    return lax.ppermute(block, axis, route)


def layer_norm(values, gain):
    centre = values - jnp.mean(values, axis=-1, keepdims=True)
    spread = jnp.mean(centre * centre, axis=-1, keepdims=True)
    return centre * lax.rsqrt(spread + 1e-06) * gain


def shards(images, w_qkv, qk_gain, w_out, in_gain, out_gain):
    section = lax.axis_index("section")
    member = lax.axis_index("tensor")
    sections = lax.axis_size("section")
    micro = images.shape[0]
    rows = images.shape[1]
    width = w_qkv.shape[2]
    span = w_out.shape[2]
    local_inner = w_qkv.shape[3]
    heads_here = local_inner // HEAD
    weights = w_qkv[0]
    outward = w_out[0]
    gain_query = qk_gain[0, 0].reshape(heads_here, HEAD)
    gain_key = qk_gain[0, 1].reshape(heads_here, HEAD)
    norm_gain = in_gain[0]

    def add_piece(piece):
        return jnp.dot(piece, outward, preferred_element_type=jnp.float32)

    def attend(state):
        normed = layer_norm(state.astype(jnp.float32), norm_gain).astype(jnp.bfloat16)
        proj = jnp.einsum("td,cde->cte", normed, weights, preferred_element_type=jnp.float32)
        query = layer_norm(proj[0].reshape(rows, heads_here, HEAD), gain_query).astype(jnp.bfloat16)
        keys = layer_norm(proj[1].reshape(rows, heads_here, HEAD), gain_key).astype(jnp.bfloat16)
        values = proj[2].astype(jnp.bfloat16).reshape(rows, heads_here, HEAD)
        scores = jnp.einsum(
            "qhe,khe->hqk", query, keys, preferred_element_type=jnp.float32
        ) * HEAD ** (-0.5)
        expo = jnp.exp(scores)
        probs = (expo / jnp.sum(expo, axis=-1, keepdims=True)).astype(jnp.bfloat16)
        att = jnp.einsum("hqk,khe->qhe", probs, values, preferred_element_type=jnp.float32)
        att = att.astype(jnp.bfloat16).reshape(rows, local_inner)
        added = add_piece(lax.all_gather(att, "tensor", axis=1, tiled=True))
        own = lax.dynamic_slice_in_dim(state, member * span, span, 1).astype(jnp.float32)
        return (own + added).astype(jnp.bfloat16)

    def pick_input(source, tick):
        index = jnp.clip(tick, 0, micro - 1).astype(jnp.int32)
        return lax.dynamic_index_in_dim(source, index, 0, keepdims=False)

    def record(buffer, tick, vector):
        index = tick - section
        valid = jnp.logical_and(index >= 0, index < micro)
        slot = jnp.clip(index, 0, micro - 1)
        previous = lax.dynamic_index_in_dim(buffer, slot, 0, keepdims=True)
        update = jnp.where(valid, vector[None, :], previous)
        return update

    buffer = jnp.zeros((micro, span), jnp.float32)
    ticks = micro + sections - 1
    full_images = lax.all_gather(images, "tensor", axis=2, tiled=True)

    def step_full(tick, carry):
        incoming, stored = carry
        state = jnp.where(section == 0, pick_input(full_images, tick), incoming)
        shard = attend(state)
        whole = lax.all_gather(shard, "tensor", axis=1, tiled=True)
        average = jnp.mean(whole.astype(jnp.float32), axis=0)
        normal = layer_norm(average, jnp.ones((width,), jnp.float32))
        vector = lax.dynamic_slice_in_dim(normal, member * span, span, 0) * out_gain
        stored = record(stored, tick, vector)
        passed = shifted(whole, "section", 1)
        return (passed, stored)

    start_rows = jnp.zeros((rows, width), jnp.bfloat16)
    final_rows, buffer = lax.fori_loop(0, ticks, step_full, (start_rows, buffer))
    return buffer[None]


def solution(mesh):
    return jax.shard_map(
        shards,
        mesh=mesh,
        in_specs=(
            P("groups", None, "tensor"),
            P("section", None, None, "tensor"),
            P("section", None, "tensor"),
            P("section", None, "tensor"),
            P("section", None),
            P("tensor"),
        ),
        out_specs=P("section", "groups", "tensor"),
        check_vma=False,
    )
```

profile of v0, /device:TPU:25, one launch (start us, length us, event | category | flops | bytes accessed | tf_op | source)
XLA Modules:
  0.0 142.3 jit_solution(4317801833432611873)
XLA Ops:
  0.8 6.3 %all_gather.21 = bf16[1,32,3072]{2,1,0:T(8,128)(2,1)S(1)} all-gather(bf16[1,32,768]{2,1,0:T(8,128)(2,1)} %param.8), channel_id=1, replica_groups=mesh['groups'=2,'section'=4,'tensor'=4] {'tensor'}, dimensions={2}, use_global_device_ids=true | all-gather | bytes 245760 | tf_op jit(solution)/shard_map/all_gather | solution.py:71
  7.1 134.7 %while.18 = (s32[]{:T(128)}, bf16[32,3072]{1,0:T(8,128)(2,1)S(1)}, f32[1,768]{1,0:T(1,128)S(1)}, pred[]{:T(512)}, bf16[1,32,3072]{2,1,0:T(8,128)(2,1)S(1)}, /*in...) while((s32[]{:T(128)}, bf16[32,3072]{1,0:T(8,128)(2,1)S(1)}, ...), condition=%wide.region_11.12_spmd.clone, body=%wide.region_0.11_spmd.clone.sunk | while | flops 609049792 | bytes 24236536 | solution.py:86
  7.6 7.6 %convolution_bitcast_fusion.2 = f32[3,32,768]{2,1,0:T(8,128)S(1)} fusion(bf16[3,3072,768]{2,1,0:T(8,128)(2,1)} %get-tuple-element.508, bf16[32,3072]{1,0:T(8,128)(2,1)S(1)} %get-tuple-element.455, f32[3072]{0:T(1024)} %bitcast.36, f32[32]{0:T(128)S(1)} %add_rsqrt_fusion.6, f32[32]{0:T(128)S(1)} %broadcast_multiply_fusion.6), kind=kOutput, calls=%fused_computation.clone.1 | convolution fusion | flops 453476352 | bytes 14659840 | tf_op jit(solution)/shard_map/while/body/eval_jaxpr/td,cde->cte/dot_general | solution.py:42
  17.6 5.6 %all_gather.26 = bf16[32,3072]{1,0:T(8,128)(2,1)S(1)} all-gather(bf16[32,768]{1,0:T(8,128)(2,1)S(1)} %reshape.97), channel_id=1, replica_groups=mesh['groups'=2,'section'=4,'tensor'=4] {'tensor'}, dimensions={1}, use_global_device_ids=true | all-gather | bytes 245760 | tf_op jit(solution)/shard_map/while/body/eval_jaxpr/all_gather | solution.py:53
  23.2 3.2 %fusion.58 = bf16[32,768]{1,0:T(8,128)(2,1)S(1)} fusion(bf16[32,3072]{1,0:T(8,128)(2,1)S(1)} %all_gather.26, bf16[3072,768]{1,0:T(8,128)(2,1)} %get-tuple-element.511, bf16[32,3072]{1,0:T(8,128)(2,1)S(1)} %get-tuple-element.455, s32[]{:T(128)} %get-tuple-element.506), kind=kOutput, calls=%fused_computation.6.clone.1 | convolution fusion | flops 151068672 | bytes 5013508 | tf_op jit(solution)/shard_map/while/body/eval_jaxpr/dot_general | solution.py:38
  26.4 5.6 %all_gather.27 = bf16[32,3072]{1,0:T(8,128)(2,1)S(1)} all-gather(bf16[32,768]{1,0:T(8,128)(2,1)S(1)} %fusion.58), channel_id=1, replica_groups=mesh['groups'=2,'section'=4,'tensor'=4] {'tensor'}, dimensions={1}, use_global_device_ids=true | all-gather | bytes 245760 | tf_op jit(solution)/shard_map/while/body/eval_jaxpr/all_gather | solution.py:77
  32.0 1.3 collective-permute-start
  36.1 4.1 %collective-permute-done = bf16[32,3072]{1,0:T(8,128)(2,1)S(1)} collective-permute-done((bf16[32,3072]{1,0:T(8,128)(2,1)S(1)}, bf16[32,3072]{1,0:T(8,128)(2,1)S(1)}, u32[]{:S(2)}, u32[]{:S(2)}) %collective-permute-start) | collective-permute-done | bytes 196640 | tf_op jit(solution)/shard_map/while/body/eval_jaxpr/ppermute | solution.py:12
  40.6 7.6 %convolution_bitcast_fusion.2 = f32[3,32,768]{2,1,0:T(8,128)S(1)} fusion(bf16[3,3072,768]{2,1,0:T(8,128)(2,1)} %get-tuple-element.508, bf16[32,3072]{1,0:T(8,128)(2,1)S(1)} %get-tuple-element.455, f32[3072]{0:T(1024)} %bitcast.36, f32[32]{0:T(128)S(1)} %add_rsqrt_fusion.6, f32[32]{0:T(128)S(1)} %broadcast_multiply_fusion.6), kind=kOutput, calls=%fused_computation.clone.1 | convolution fusion | flops 453476352 | bytes 14659840 | tf_op jit(solution)/shard_map/while/body/eval_jaxpr/td,cde->cte/dot_general | solution.py:42
  50.6 6.5 %all_gather.26 = bf16[32,3072]{1,0:T(8,128)(2,1)S(1)} all-gather(bf16[32,768]{1,0:T(8,128)(2,1)S(1)} %reshape.97), channel_id=1, replica_groups=mesh['groups'=2,'section'=4,'tensor'=4] {'tensor'}, dimensions={1}, use_global_device_ids=true | all-gather | bytes 245760 | tf_op jit(solution)/shard_map/while/body/eval_jaxpr/all_gather | solution.py:53
  57.0 3.2 %fusion.58 = bf16[32,768]{1,0:T(8,128)(2,1)S(1)} fusion(bf16[32,3072]{1,0:T(8,128)(2,1)S(1)} %all_gather.26, bf16[3072,768]{1,0:T(8,128)(2,1)} %get-tuple-element.511, bf16[32,3072]{1,0:T(8,128)(2,1)S(1)} %get-tuple-element.455, s32[]{:T(128)} %get-tuple-element.506), kind=kOutput, calls=%fused_computation.6.clone.1 | convolution fusion | flops 151068672 | bytes 5013508 | tf_op jit(solution)/shard_map/while/body/eval_jaxpr/dot_general | solution.py:38
  60.2 5.6 %all_gather.27 = bf16[32,3072]{1,0:T(8,128)(2,1)S(1)} all-gather(bf16[32,768]{1,0:T(8,128)(2,1)S(1)} %fusion.58), channel_id=1, replica_groups=mesh['groups'=2,'section'=4,'tensor'=4] {'tensor'}, dimensions={1}, use_global_device_ids=true | all-gather | bytes 245760 | tf_op jit(solution)/shard_map/while/body/eval_jaxpr/all_gather | solution.py:77
  65.8 1.3 collective-permute-start
  70.0 4.1 %collective-permute-done = bf16[32,3072]{1,0:T(8,128)(2,1)S(1)} collective-permute-done((bf16[32,3072]{1,0:T(8,128)(2,1)S(1)}, bf16[32,3072]{1,0:T(8,128)(2,1)S(1)}, u32[]{:S(2)}, u32[]{:S(2)}) %collective-permute-start) | collective-permute-done | bytes 196640 | tf_op jit(solution)/shard_map/while/body/eval_jaxpr/ppermute | solution.py:12
  74.4 7.6 %convolution_bitcast_fusion.2 = f32[3,32,768]{2,1,0:T(8,128)S(1)} fusion(bf16[3,3072,768]{2,1,0:T(8,128)(2,1)} %get-tuple-element.508, bf16[32,3072]{1,0:T(8,128)(2,1)S(1)} %get-tuple-element.455, f32[3072]{0:T(1024)} %bitcast.36, f32[32]{0:T(128)S(1)} %add_rsqrt_fusion.6, f32[32]{0:T(128)S(1)} %broadcast_multiply_fusion.6), kind=kOutput, calls=%fused_computation.clone.1 | convolution fusion | flops 453476352 | bytes 14659840 | tf_op jit(solution)/shard_map/while/body/eval_jaxpr/td,cde->cte/dot_general | solution.py:42
  84.4 6.5 %all_gather.26 = bf16[32,3072]{1,0:T(8,128)(2,1)S(1)} all-gather(bf16[32,768]{1,0:T(8,128)(2,1)S(1)} %reshape.97), channel_id=1, replica_groups=mesh['groups'=2,'section'=4,'tensor'=4] {'tensor'}, dimensions={1}, use_global_device_ids=true | all-gather | bytes 245760 | tf_op jit(solution)/shard_map/while/body/eval_jaxpr/all_gather | solution.py:53
  90.9 3.2 %fusion.58 = bf16[32,768]{1,0:T(8,128)(2,1)S(1)} fusion(bf16[32,3072]{1,0:T(8,128)(2,1)S(1)} %all_gather.26, bf16[3072,768]{1,0:T(8,128)(2,1)} %get-tuple-element.511, bf16[32,3072]{1,0:T(8,128)(2,1)S(1)} %get-tuple-element.455, s32[]{:T(128)} %get-tuple-element.506), kind=kOutput, calls=%fused_computation.6.clone.1 | convolution fusion | flops 151068672 | bytes 5013508 | tf_op jit(solution)/shard_map/while/body/eval_jaxpr/dot_general | solution.py:38
  94.1 5.6 %all_gather.27 = bf16[32,3072]{1,0:T(8,128)(2,1)S(1)} all-gather(bf16[32,768]{1,0:T(8,128)(2,1)S(1)} %fusion.58), channel_id=1, replica_groups=mesh['groups'=2,'section'=4,'tensor'=4] {'tensor'}, dimensions={1}, use_global_device_ids=true | all-gather | bytes 245760 | tf_op jit(solution)/shard_map/while/body/eval_jaxpr/all_gather | solution.py:77
  103.8 4.1 %collective-permute-done = bf16[32,3072]{1,0:T(8,128)(2,1)S(1)} collective-permute-done((bf16[32,3072]{1,0:T(8,128)(2,1)S(1)}, bf16[32,3072]{1,0:T(8,128)(2,1)S(1)}, u32[]{:S(2)}, u32[]{:S(2)}) %collective-permute-start) | collective-permute-done | bytes 196640 | tf_op jit(solution)/shard_map/while/body/eval_jaxpr/ppermute | solution.py:12
  108.3 7.6 %convolution_bitcast_fusion.2 = f32[3,32,768]{2,1,0:T(8,128)S(1)} fusion(bf16[3,3072,768]{2,1,0:T(8,128)(2,1)} %get-tuple-element.508, bf16[32,3072]{1,0:T(8,128)(2,1)S(1)} %get-tuple-element.455, f32[3072]{0:T(1024)} %bitcast.36, f32[32]{0:T(128)S(1)} %add_rsqrt_fusion.6, f32[32]{0:T(128)S(1)} %broadcast_multiply_fusion.6), kind=kOutput, calls=%fused_computation.clone.1 | convolution fusion | flops 453476352 | bytes 14659840 | tf_op jit(solution)/shard_map/while/body/eval_jaxpr/td,cde->cte/dot_general | solution.py:42
  118.3 6.5 %all_gather.26 = bf16[32,3072]{1,0:T(8,128)(2,1)S(1)} all-gather(bf16[32,768]{1,0:T(8,128)(2,1)S(1)} %reshape.97), channel_id=1, replica_groups=mesh['groups'=2,'section'=4,'tensor'=4] {'tensor'}, dimensions={1}, use_global_device_ids=true | all-gather | bytes 245760 | tf_op jit(solution)/shard_map/while/body/eval_jaxpr/all_gather | solution.py:53
  124.8 3.2 %fusion.58 = bf16[32,768]{1,0:T(8,128)(2,1)S(1)} fusion(bf16[32,3072]{1,0:T(8,128)(2,1)S(1)} %all_gather.26, bf16[3072,768]{1,0:T(8,128)(2,1)} %get-tuple-element.511, bf16[32,3072]{1,0:T(8,128)(2,1)S(1)} %get-tuple-element.455, s32[]{:T(128)} %get-tuple-element.506), kind=kOutput, calls=%fused_computation.6.clone.1 | convolution fusion | flops 151068672 | bytes 5013508 | tf_op jit(solution)/shard_map/while/body/eval_jaxpr/dot_general | solution.py:38
  128.0 5.6 %all_gather.27 = bf16[32,3072]{1,0:T(8,128)(2,1)S(1)} all-gather(bf16[32,768]{1,0:T(8,128)(2,1)S(1)} %fusion.58), channel_id=1, replica_groups=mesh['groups'=2,'section'=4,'tensor'=4] {'tensor'}, dimensions={1}, use_global_device_ids=true | all-gather | bytes 245760 | tf_op jit(solution)/shard_map/while/body/eval_jaxpr/all_gather | solution.py:77
  137.7 4.1 %collective-permute-done = bf16[32,3072]{1,0:T(8,128)(2,1)S(1)} collective-permute-done((bf16[32,3072]{1,0:T(8,128)(2,1)S(1)}, bf16[32,3072]{1,0:T(8,128)(2,1)S(1)}, u32[]{:S(2)}, u32[]{:S(2)}) %collective-permute-start) | collective-permute-done | bytes 196640 | tf_op jit(solution)/shard_map/while/body/eval_jaxpr/ppermute | solution.py:12
  (139 shorter events, 20.5 us)
Async XLA Ops:
  7.1 28.9 %copy-start = (f32[768]{0:T(1024)S(1)}, f32[768]{0:T(1024)}, u32[]{:S(2)}) copy-start(f32[768]{0:T(1024)} %get-tuple-element.513) | copy-start | bytes 9220 | tf_op jit(solution)/shard_map/while
  32.0 8.2 %collective-permute-start = (bf16[32,3072]{1,0:T(8,128)(2,1)S(1)}, bf16[32,3072]{1,0:T(8,128)(2,1)S(1)}, u32[]{:S(2)}, u32[]{:S(2)}) collective-permute-start(bf16[32,3072]{1,0:T(8,128)(2,1)S(1)} %all_gather.27), channel_id=1, source_target_pairs={{0,4},{4,8},{8,12},{1,5},{5,9},{9,13},{2,6},{6,10},{10,14},{3,7},{... | collective-permute-start | bytes 589832 | tf_op jit(solution)/shard_map/while/body/eval_jaxpr/ppermute | solution.py:12
  40.1 29.7 %copy-start = (f32[768]{0:T(1024)S(1)}, f32[768]{0:T(1024)}, u32[]{:S(2)}) copy-start(f32[768]{0:T(1024)} %get-tuple-element.513) | copy-start | bytes 9220 | tf_op jit(solution)/shard_map/while
  65.8 8.2 %collective-permute-start = (bf16[32,3072]{1,0:T(8,128)(2,1)S(1)}, bf16[32,3072]{1,0:T(8,128)(2,1)S(1)}, u32[]{:S(2)}, u32[]{:S(2)}) collective-permute-start(bf16[32,3072]{1,0:T(8,128)(2,1)S(1)} %all_gather.27), channel_id=1, source_target_pairs={{0,4},{4,8},{8,12},{1,5},{5,9},{9,13},{2,6},{6,10},{10,14},{3,7},{... | collective-permute-start | bytes 589832 | tf_op jit(solution)/shard_map/while/body/eval_jaxpr/ppermute | solution.py:12
  74.0 29.7 %copy-start = (f32[768]{0:T(1024)S(1)}, f32[768]{0:T(1024)}, u32[]{:S(2)}) copy-start(f32[768]{0:T(1024)} %get-tuple-element.513) | copy-start | bytes 9220 | tf_op jit(solution)/shard_map/while
  99.7 8.2 %collective-permute-start = (bf16[32,3072]{1,0:T(8,128)(2,1)S(1)}, bf16[32,3072]{1,0:T(8,128)(2,1)S(1)}, u32[]{:S(2)}, u32[]{:S(2)}) collective-permute-start(bf16[32,3072]{1,0:T(8,128)(2,1)S(1)} %all_gather.27), channel_id=1, source_target_pairs={{0,4},{4,8},{8,12},{1,5},{5,9},{9,13},{2,6},{6,10},{10,14},{3,7},{... | collective-permute-start | bytes 589832 | tf_op jit(solution)/shard_map/while/body/eval_jaxpr/ppermute | solution.py:12
  107.9 29.7 %copy-start = (f32[768]{0:T(1024)S(1)}, f32[768]{0:T(1024)}, u32[]{:S(2)}) copy-start(f32[768]{0:T(1024)} %get-tuple-element.513) | copy-start | bytes 9220 | tf_op jit(solution)/shard_map/while
  133.6 8.2 %collective-permute-start = (bf16[32,3072]{1,0:T(8,128)(2,1)S(1)}, bf16[32,3072]{1,0:T(8,128)(2,1)S(1)}, u32[]{:S(2)}, u32[]{:S(2)}) collective-permute-start(bf16[32,3072]{1,0:T(8,128)(2,1)S(1)} %all_gather.27), channel_id=1, source_target_pairs={{0,4},{4,8},{8,12},{1,5},{5,9},{9,13},{2,6},{6,10},{10,14},{3,7},{... | collective-permute-start | bytes 589832 | tf_op jit(solution)/shard_map/while/body/eval_jaxpr/ppermute | solution.py:12
  141.8 0.6 copy-start.1
where the time goes:
time: 144 us; the launch traced here: 142 us
  blocking collectives  53.6 us (37%)
  matrix products  45 us (31%)
  waiting for transfers between devices  16.2 us (11%)
  other arithmetic  12.2 us (8%)
  loops' own time  6.02 us (4%)
  starting transfers between devices  5.12 us (4%)
  local copies, waits for them, and re-layouts  4.09 us (3%)
    dot_general x4, matrix products, attend(): jnp.einsum('td,cde->cte', normed, weights, preferred_element_type=jnp.flo...  30.5 us
    all_gather x4, blocking collectives, attend(): added = add_piece(lax.all_gather(att, 'tensor', axis=1, tiled=True))  25 us
    all_gather x4, blocking collectives, step_full(): whole = lax.all_gather(shard, 'tensor', axis=1, tiled=True)  22.4 us
    ppermute x4, waiting for transfers between devices, shifted(): return lax.ppermute(block, axis, route)  16.2 us
    dot_general x4, matrix products, add_piece(): return jnp.dot(piece, outward, preferred_element_type=jnp.float32)  12.8 us
    all_gather x1, blocking collectives, shards(): full_images = lax.all_gather(images, 'tensor', axis=2, tiled=True)  6.3 us
    another operation x1, loops' own time, shards(): lax.fori_loop(0, ticks, step_full, (start_rows, buffer))  6.02 us
    reduce_sum x16, other arithmetic, layer_norm(): spread = jnp.mean(centre * centre, axis=-1, keepdims=True)  5.53 us
  transfers between devices with their start and end apart: 4, of which 4 were waited for; matrix products, arithmetic and copies ran while one was open for 4% of the time, Pallas kernels for 0%

commit v1 on v0

v1 whole, which is shorter than its diff:
```python
import functools

import jax
import jax.numpy as jnp
from jax import lax
from jax.experimental import pallas as pl
from jax.experimental.pallas import tpu as pltpu
from jax.sharding import PartitionSpec as P

HEAD = 64
EPS = 1e-06
MESH = pl.DeviceIdType.MESH


def remote(src, dst, send_sem, recv_sem, section, member):
    return pltpu.make_async_remote_copy(
        src_ref=src,
        dst_ref=dst,
        send_sem=send_sem,
        recv_sem=recv_sem,
        device_id={"section": section, "tensor": member},
        device_id_type=MESH,
    )


def block_mean(values, averager):
    high = values.astype(jnp.bfloat16)
    low = (values - high.astype(jnp.float32)).astype(jnp.bfloat16)
    return jnp.dot(high, averager, preferred_element_type=jnp.float32) + jnp.dot(
        low, averager, preferred_element_type=jnp.float32
    )


def kernel(
    sections,
    n,
    images,
    w_qkv,
    qk_gain,
    w_out,
    in_gain,
    pooled,
    wq,
    wo,
    gains,
    norm_gain,
    state,
    att,
    fresh,
    stats,
    w_sem,
    wo_sem,
    gain_sem,
    x_send,
    x_fwd,
    x_recv,
    a_send,
    a_fwd,
    a_recv,
    y_send,
    s_send,
    s_recv,
):
    section = lax.axis_index("section")
    me = lax.axis_index("tensor")
    chips = n // 2
    core = lax.rem(me, 2)
    chip = me // 2
    sibling = chip * 2 + 1 - core
    rows, span = fresh.shape
    inner = att.shape[2]
    width = n * span
    first = section == 0
    last = section == sections - 1

    def member_of(k):
        return lax.rem(chip + k, chips) * 2 + core

    image_copy = pltpu.make_async_copy(images.at[0], state.at[me], gain_sem.at[2])

    @pl.when(first)
    def _():
        image_copy.start()

    gain_copies = [
        pltpu.make_async_copy(in_gain, norm_gain, gain_sem.at[0]),
        pltpu.make_async_copy(qk_gain.at[0], gains, gain_sem.at[1]),
    ]
    for copy in gain_copies:
        copy.start()
    w_copies = [
        pltpu.make_async_copy(
            w_qkv.at[0, :, pl.ds(j * span, span), :], wq.at[:, pl.ds(j * span, span), :], w_sem.at[j]
        )
        for j in range(n)
    ]
    for copy in w_copies:
        copy.start()
    wo_copy = pltpu.make_async_copy(w_out.at[0], wo, wo_sem)
    wo_copy.start()

    barrier = pltpu.get_barrier_semaphore()
    for k in range(1, n):
        pl.semaphore_signal(
            barrier, inc=1, device_id={"section": section, "tensor": lax.rem(me + k, n)}, device_id_type=MESH
        )

    @pl.when(jnp.logical_not(first))
    def _():
        for k in range(chips):
            pl.semaphore_signal(
                barrier, inc=1, device_id={"section": section - 1, "tensor": member_of(k)}, device_id_type=MESH
            )

    @pl.when(jnp.logical_not(last))
    def _():
        for k in range(chips):
            pl.semaphore_signal(
                barrier, inc=1, device_id={"section": section + 1, "tensor": member_of(k)}, device_id_type=MESH
            )

    neighbours = (section > 0).astype(jnp.int32) + (section < sections - 1).astype(jnp.int32)
    pl.semaphore_wait(barrier, n - 1 + chips * neighbours)

    def outgoing(buffer, send, recv):
        copies = [
            remote(buffer.at[me], buffer.at[me], send.at[k], recv.at[me], section, member_of(k))
            for k in range(1, chips)
        ]
        copies.append(remote(buffer.at[me], buffer.at[me], send.at[0], recv.at[me], section, sibling))
        return copies

    def relay(buffer, fwd, recv, k):
        piece = member_of(k)
        return remote(buffer.at[piece], buffer.at[piece], fwd.at[k], recv.at[piece], section, sibling)

    def arrival(buffer, send, recv, piece):
        return remote(buffer.at[piece], buffer.at[piece], send.at[0], recv.at[piece], section, sibling)

    def gather(buffer, send, fwd, recv):
        for k in range(1, chips):
            arrival(buffer, send, recv, member_of(k)).wait_recv()
            relay(buffer, fwd, recv, k).start()
        for k in range(chips):
            arrival(buffer, send, recv, lax.rem(chip + k, chips) * 2 + 1 - core).wait_recv()

    @pl.when(first)
    def _():
        image_copy.wait()
        for copy in outgoing(state, x_send, x_recv):
            copy.start()
        gather(state, x_send, x_fwd, x_recv)

    @pl.when(jnp.logical_not(first))
    def _():
        for k in range(chips):
            arrival(state, x_send, x_recv, member_of(k)).wait_recv()
            relay(state, x_fwd, x_recv, k).start()
        for k in range(chips):
            arrival(state, x_send, x_recv, lax.rem(chip + k, chips) * 2 + 1 - core).wait_recv()

    for copy in gain_copies:
        copy.wait()

    pieces = [state[j].astype(jnp.float32) for j in range(n)]
    total = pieces[0].sum(axis=-1, keepdims=True)
    for j in range(1, n):
        total = total + pieces[j].sum(axis=-1, keepdims=True)
    mean = total * (1.0 / width)
    spread = jnp.zeros_like(mean)
    for j in range(n):
        centre = pieces[j] - mean
        spread = spread + (centre * centre).sum(axis=-1, keepdims=True)
    scale = lax.rsqrt(spread * (1.0 / width) + EPS)
    proj = [None, None, None]
    for j in range(n):
        gain = norm_gain[:, j * span : (j + 1) * span]
        normed = ((pieces[j] - mean) * scale * gain).astype(jnp.bfloat16)
        w_copies[j].wait()
        for c in range(3):
            part = jnp.dot(normed, wq[c, j * span : (j + 1) * span, :], preferred_element_type=jnp.float32)
            proj[c] = part if proj[c] is None else proj[c] + part

    block = 2 * HEAD if inner % (2 * HEAD) == 0 else HEAD
    blocks = inner // block
    pair = block // HEAD
    side_rows = lax.broadcasted_iota(jnp.int32, (block, block), 0) < HEAD
    side_columns = lax.broadcasted_iota(jnp.int32, (block, block), 1) < HEAD
    averager = jnp.where(side_rows == side_columns, 1.0 / HEAD, 0.0).astype(jnp.bfloat16)
    stacked = jnp.concatenate(
        [proj[c][:, b * block : (b + 1) * block] for c in range(2) for b in range(blocks)], axis=0
    )
    centre = stacked - block_mean(stacked, averager)
    factor = lax.rsqrt(block_mean(centre * centre, averager) + EPS)
    normal = centre * factor
    left = lax.broadcasted_iota(jnp.int32, (rows, block), 1) < HEAD
    scores = []
    for b in range(blocks):
        lanes = slice(b * block, (b + 1) * block)
        query = (normal[b * rows : (b + 1) * rows] * gains[0:1, lanes]).astype(jnp.bfloat16)
        at = (blocks + b) * rows
        keys = (normal[at : at + rows] * gains[1:2, lanes]).astype(jnp.bfloat16)
        if pair == 2:
            zero = jnp.zeros_like(query)
            query = jnp.concatenate([jnp.where(left, query, zero), jnp.where(left, zero, query)], axis=0)
        scores.append(
            lax.dot_general(query, keys, (((1,), (1,)), ((), ())), preferred_element_type=jnp.float32)
        )
    expo = jnp.exp(jnp.concatenate(scores, axis=0) * HEAD ** (-0.5))
    probs = (expo / jnp.sum(expo, axis=-1, keepdims=True)).astype(jnp.bfloat16)
    for b in range(blocks):
        lanes = slice(b * block, (b + 1) * block)
        values = proj[2][:, lanes].astype(jnp.bfloat16)
        mixed = jnp.dot(
            probs[b * pair * rows : (b + 1) * pair * rows], values, preferred_element_type=jnp.float32
        )
        if pair == 2:
            mixed = jnp.where(left, mixed[:rows], mixed[rows:])
        att[me, :, lanes] = mixed.astype(jnp.bfloat16)

    for copy in outgoing(att, a_send, a_recv):
        copy.start()
    gather(att, a_send, a_fwd, a_recv)
    wo_copy.wait()
    added = state[me].astype(jnp.float32)
    update = None
    for j in range(n):
        part = jnp.dot(att[j], wo[j * inner : (j + 1) * inner, :], preferred_element_type=jnp.float32)
        update = part if update is None else update + part
    whole = (added + update).astype(jnp.bfloat16)
    fresh[...] = whole

    def onward(k):
        return remote(fresh, state.at[me], y_send.at[k], x_recv.at[me], section + 1, member_of(k))

    @pl.when(jnp.logical_not(last))
    def _():
        for k in range(chips):
            onward((k + 1) % chips).start()

    average = jnp.sum(whole.astype(jnp.float32), axis=0, keepdims=True) * (1.0 / rows)
    local_mean = jnp.sum(average, axis=-1, keepdims=True) * (1.0 / span)
    off = average - local_mean
    local_spread = jnp.sum(off * off, axis=-1, keepdims=True)
    shape = stats.shape[2:]
    stats[me, 0] = jnp.broadcast_to(local_mean, shape)
    stats[me, 1] = jnp.broadcast_to(local_spread, shape)
    stat_copies = [
        remote(stats.at[me], stats.at[me], s_send.at[k], s_recv.at[me], section, lax.rem(me + k, n))
        for k in range(1, n)
    ]
    for copy in stat_copies:
        copy.start()
    for k in range(1, n):
        arrival(stats, s_send, s_recv, lax.rem(me + k, n)).wait_recv()
    centre_all = stats[0, 0]
    for j in range(1, n):
        centre_all = centre_all + stats[j, 0]
    centre_all = centre_all * (1.0 / n)
    spread_all = jnp.zeros(shape, jnp.float32)
    for j in range(n):
        gap = stats[j, 0] - centre_all
        spread_all = spread_all + (stats[j, 1] + span * (gap * gap))
    factor = lax.rsqrt(spread_all * (1.0 / width) + EPS)
    pooled[...] = (average - centre_all[0:1, 0:1]) * factor[0:1, 0:1]

    @pl.when(first)
    def _():
        for copy in outgoing(state, x_send, x_recv):
            copy.wait_send()

    @pl.when(jnp.logical_not(first))
    def _():
        relay(state, x_fwd, x_recv, 0).wait_send()

    for k in range(1, chips):
        relay(state, x_fwd, x_recv, k).wait_send()
        relay(att, a_fwd, a_recv, k).wait_send()
    for copy in outgoing(att, a_send, a_recv):
        copy.wait_send()
    for copy in stat_copies:
        copy.wait_send()

    @pl.when(jnp.logical_not(last))
    def _():
        for k in range(chips):
            onward(k).wait_send()


def solution(mesh):
    sections, n = mesh.shape["section"], mesh.shape["tensor"]

    def shards(images, w_qkv, qk_gain, w_out, in_gain, out_gain):
        rows, span = images.shape[1], images.shape[2]
        width, inner = w_qkv.shape[2], w_qkv.shape[3]
        dma = pltpu.SemaphoreType.DMA
        normal = pl.pallas_call(
            functools.partial(kernel, sections, n),
            out_shape=jax.ShapeDtypeStruct((1, span), jnp.float32),
            in_specs=[pl.BlockSpec(memory_space=pl.ANY)] * 5,
            out_specs=pl.BlockSpec(memory_space=pltpu.VMEM),
            scratch_shapes=[
                pltpu.VMEM((3, width, inner), jnp.bfloat16),
                pltpu.VMEM((w_out.shape[1], span), jnp.bfloat16),
                pltpu.VMEM((2, inner), jnp.float32),
                pltpu.VMEM((1, width), jnp.float32),
                pltpu.VMEM((n, rows, span), jnp.bfloat16),
                pltpu.VMEM((n, rows, inner), jnp.bfloat16),
                pltpu.VMEM((rows, span), jnp.bfloat16),
                pltpu.VMEM((n, 2, 8, 128), jnp.float32),
                dma((n,)),
                dma,
                dma((3,)),
                dma((n // 2,)),
                dma((n // 2,)),
                dma((n,)),
                dma((n // 2,)),
                dma((n // 2,)),
                dma((n,)),
                dma((n // 2,)),
                dma((n,)),
                dma((n,)),
            ],
            compiler_params=pltpu.CompilerParams(collective_id=0, has_side_effects=True),
        )(images, w_qkv, qk_gain, w_out, in_gain)
        return (normal * out_gain)[:, None, :]

    return jax.shard_map(
        shards,
        mesh=mesh,
        in_specs=(
            P("groups", None, "tensor"),
            P("section", None, None, "tensor"),
            P("section", None, "tensor"),
            P("section", None, "tensor"),
            P("section", None),
            P("tensor"),
        ),
        out_specs=P("section", "groups", "tensor"),
        check_vma=False,
    )
```

time: 144 us -> 59.5 us (0.41)
  Pallas kernels: 0 us -> 57.3 us
  blocking collectives: 53.6 us -> 0 us
  matrix products: 45 us -> 0 us
  waiting for transfers between devices: 16.2 us -> 0 us
  other arithmetic: 12.2 us -> 1.25 us
  loops' own time: 6.02 us -> 0 us
  starting transfers between devices: 5.12 us -> 0 us
  local copies, waits for them, and re-layouts: 4.09 us -> 0.01 us
    pallas_call x0 -> x1, Pallas kernels: none -> 57.3 us  [shards(): pl.pallas_call(functools.partial(kernel, sections, n), out_shape=jax.Shap...]
    all_gather x9 -> x0, blocking collectives: 53.6 us -> none  [the longest x4 25 us: attend(): added = add_piece(lax.all_gather(att, 'tensor', axis=1, tiled=True))]
    dot_general x16 -> x0, matrix products: 45 us -> none  [the longest x4 30.5 us: attend(): jnp.einsum('td,cde->cte', normed, weights, preferred_element_type=jnp.flo...]
    ppermute x4 -> x0, waiting for transfers between devices: 16.2 us -> none  [shifted(): return lax.ppermute(block, axis, route)]
    reduce_sum x36 -> x0, other arithmetic: 10.2 us -> none  [the longest x16 5.53 us: layer_norm(): spread = jnp.mean(centre * centre, axis=-1, keepdims=True)]
    another operation x1 -> x0, loops' own time: 6.02 us -> none  [shards(): lax.fori_loop(0, ticks, step_full, (start_rows, buffer))]
    ppermute x4 -> x0, starting transfers between devices: 5.12 us -> none  [shifted(): return lax.ppermute(block, axis, route)]
  transfers between devices with their start and end apart: 4 -> 0, of which waited for: 4 -> 0; matrix products, arithmetic and copies ran while one was open for 4% -> 0% of each run, Pallas kernels for 0% -> 0%
where the time goes in v1:
time: 59.5 us; the launch traced here: 58.6 us
  Pallas kernels  57.3 us (96%)
  other arithmetic  1.25 us (2%)
    pallas_call x1, Pallas kernels, shards(): pl.pallas_call(functools.partial(kernel, sections, n), out_shape=jax.Shap...  57.3 us
    broadcast_in_dim x1, other arithmetic, shards(): return (normal * out_gain)[:, None, :]  1.25 us

profile of v1, /device:TPU:25, one launch (start us, length us, event | category | flops | bytes accessed | tf_op | source)
XLA Modules:
  0.0 58.6 jit_solution(16579364065544180672)
XLA Ops:
  0.0 0.0 copy-start
  0.0 57.3 %shard_map.64 = f32[1,768]{1,0:T(1,128)} custom-call(bf16[1,32,768]{2,1,0:T(8,128)(2,1)} %images.1, bf16[1,3,3072,768]{3,2,1,0:T(8,128)(2,1)} %w_qkv.1, f32[1,2,768]{2,1,0:T(2,128)} %qk_gain.1, bf16[1,3072,768]{2,1,0:T(8,128)(2,1)} %w_out.1, f32[1,3072]{1,0:T(1,128)} %in_gain.1), custom_call_target="tpu_custom_call" | custom-call | tf_op jit(solution)/shard_map/pallas_call | solution.py:297
  57.3 0.0 copy-done
  57.3 1.3 %multiply_bitcast_fusion = f32[1,1,768]{2,1,0:T(1,128)} fusion(f32[1,768]{1,0:T(1,128)} %shard_map.64, f32[768]{0:T(1024)S(1)} %copy-done), kind=kLoop, calls=%fused_computation | loop fusion | flops 768 | bytes 9216 | tf_op jit(solution)/shard_map/broadcast_in_dim | solution.py:326
Async XLA Ops:
  0.0 57.3 %copy-start = (f32[768]{0:T(1024)S(1)}, f32[768]{0:T(1024)}, u32[]{:S(2)}) copy-start(f32[768]{0:T(1024)} %param.11) | copy-start | bytes 9220
